TPU v7x, 32 devices: a whole 2x2x4 slice. The times are simulated.
32 devices in a mesh: fsdp: 4 (over y, x), dp: 8 (over z, core).
Axes of the slice: x: 2, y: 2, z: 4, core: 2. Of those that a mesh axis runs over, the one named last changes fastest.
Arguments:
- hidden_in: bfloat16 [8192, 1536], P(('fsdp', 'dp')), may hold values from -6 to 6
- lengths: int32 [32, 4], P(('fsdp', 'dp')), may hold values from 0 to 256, as said below
- norm_gain: bfloat16 [1536], P(('fsdp', 'dp')), may hold values from 0.5 to 1.5
- in_proj: bfloat16 [1536, 6448], P(('fsdp', 'dp')), may hold values from -0.15625 to 0.15625
- conv_weight: bfloat16 [3328, 4], P(('fsdp', 'dp')), may hold values from -3 to 3
- conv_bias: bfloat16 [3328], P(('fsdp', 'dp')), may hold values from -3 to 3
- gate_gain: bfloat16 [3072], P(('fsdp', 'dp')), may hold values from 0.5 to 1.5
- out_proj: bfloat16 [3072, 1536], P(('fsdp', 'dp')), may hold values from -0.109375 to 0.109375
- decay_log: float32 [48], replicated, may hold values from -3 to 1.5
- step_bias: float32 [48], replicated, may hold values from -5 to -2
- skip_gain: float32 [48], replicated, may hold values from 0.5 to 1.5
- grad_out: bfloat16 [8192, 1536], P(('fsdp', 'dp')), may hold values from -6 to 6
Outputs:
- hidden_out: bfloat16 [8192, 1536], P(('fsdp', 'dp'))
- grad_in: float32 [8192, 1536], P(('fsdp', 'dp'))
- grad_norm_gain: float32 [1536], P(('fsdp', 'dp'))
- grad_in_proj: float32 [1536, 6448], P(('fsdp', 'dp'))
- grad_conv_weight: float32 [3328, 4], P(('fsdp', 'dp'))
- grad_conv_bias: float32 [3328], P(('fsdp', 'dp'))
- grad_gate_gain: float32 [3072], P(('fsdp', 'dp'))
- grad_out_proj: float32 [3072, 1536], P(('fsdp', 'dp'))
- grad_decay_log: float32 [48], replicated
- grad_step_bias: float32 [48], replicated
- grad_skip_gain: float32 [48], replicated
Inputs may be any that keep to these rules, and one draw needn't show every extreme that they name: lengths[b] lists the sequences packed from the first row of block b on, in order; a length may be 0 (an empty slot); each block's lengths sum to at most 256 and the rows after that sum are padding; in every draw one block holds a single sequence of exactly 256 rows.
All inputs are finite; a program needn't handle non-finite values.
Results may differ from a plain program's by a relative error of at most 0.0063.
Values may be sent and summed in bfloat16 or wider, within the bound.
A program may use at most 192 MiB of HBM per device.

v0:
```python
import jax
import jax.numpy as jnp
from jax import lax
from jax.sharding import PartitionSpec as P

SPAN = 256
EPS = 1e-05
full_precision = lax.Precision.HIGHEST


def segment_ids(lens_row, row_count):
    ends = jnp.cumsum(lens_row)
    places = jnp.arange(row_count, dtype=jnp.int32)
    seg_ids = jnp.sum((places[:, None] >= ends[None, :]).astype(jnp.int32), axis=1)
    valid = (seg_ids < lens_row.shape[0]).astype(jnp.float32)
    return (seg_ids, valid)


def pre_norm(values, weight):
    return (
        values * lax.rsqrt(jnp.mean(values * values, axis=1, keepdims=True) + EPS) * weight[None, :]
    )


def convolve(inputs, weight, bias_row, seg_ids):
    kernel_len = weight.shape[1]
    summed = bias_row[None, :] + inputs * weight[:, kernel_len - 1][None, :]
    for offset in range(1, kernel_len):
        shifted = jnp.pad(inputs, ((offset, 0), (0, 0)))[:-offset]
        earlier = jnp.pad(seg_ids, (offset, 0), constant_values=-1)[:-offset]
        keep_mask = (earlier == seg_ids).astype(jnp.float32)
        summed = summed + shifted * keep_mask[:, None] * weight[:, kernel_len - 1 - offset][None, :]
    return summed


def state_scan(x_act, steps_dt, decay_rate, b_mat, c_mat, skips, seg_ids):
    row_count = x_act.shape[0]
    head_count = steps_dt.shape[1]
    head_dim = x_act.shape[1] // head_count
    state_dim = b_mat.shape[1]
    blocks = row_count // SPAN
    x_blocks = x_act.reshape(blocks, SPAN, head_count, head_dim)
    dt_blocks = steps_dt.reshape(blocks, SPAN, head_count)
    b_blocks = b_mat.reshape(blocks, SPAN, state_dim)
    c_blocks = c_mat.reshape(blocks, SPAN, state_dim)
    seg_blocks = seg_ids.reshape(blocks, SPAN)
    lower_tri = jnp.arange(SPAN)[:, None] >= jnp.arange(SPAN)[None, :]

    def block_step(scan_carry, block_in):
        old_state, prev_seg = scan_carry
        x_blk, dt_blk, b_blk, c_blk, seg_blk = block_in
        log_decay = jnp.cumsum(dt_blk * decay_rate[None, :], axis=0)
        same_seq = (seg_blk[:, None] == seg_blk[None, :]) & lower_tri
        spread = log_decay.T[:, :, None] - log_decay.T[:, None, :]
        decays = jnp.exp(jnp.where(same_seq[None], spread, -jnp.inf))
        inner_cb = jnp.dot(c_blk, b_blk.T, precision=full_precision)
        mixing = decays * inner_cb[None] * dt_blk.T[:, None, :]
        result = jnp.einsum("hts,shp->thp", mixing, x_blk, precision=full_precision)
        enters = (seg_blk == prev_seg).astype(jnp.float32)
        carried = jnp.einsum("tn,hpn->thp", c_blk, old_state, precision=full_precision)
        result = result + jnp.exp(log_decay)[:, :, None] * enters[:, None, None] * carried
        result = result + skips[None, :, None] * x_blk
        last_seg = seg_blk[-1]
        tail_wts = (
            jnp.exp(log_decay[-1][None, :] - log_decay)
            * (seg_blk == last_seg).astype(jnp.float32)[:, None]
            * dt_blk
        )
        new_state = jnp.einsum("sh,shp,sn->hpn", tail_wts, x_blk, b_blk, precision=full_precision)
        keep_old = jnp.exp(log_decay[-1]) * (prev_seg == last_seg).astype(jnp.float32)
        new_state = new_state + keep_old[:, None, None] * old_state
        return ((new_state, last_seg), result)

    start_state = (
        jnp.zeros((head_count, head_dim, state_dim), jnp.float32),
        jnp.array(-1, jnp.int32),
    )
    _, outputs = lax.scan(
        jax.checkpoint(block_step),
        start_state,
        (x_blocks, dt_blocks, b_blocks, c_blocks, seg_blocks),
    )
    return outputs.reshape(row_count, head_count * head_dim)


def mixer_branch(projected, kernel, shift_bias, gate, rates, biases, skips, seg_ids, valid):
    inner_dim = gate.shape[0]
    conv_dim = shift_bias.shape[0]
    state_dim = (conv_dim - inner_dim) // 2
    gate_in = projected[:, :inner_dim]
    conv_in = projected[:, inner_dim : inner_dim + conv_dim]
    dt_raw = projected[:, inner_dim + conv_dim :]
    activ = jax.nn.silu(convolve(conv_in, kernel, shift_bias, seg_ids))
    x_act = activ[:, :inner_dim]
    b_mat = activ[:, inner_dim : inner_dim + state_dim]
    c_mat = activ[:, inner_dim + state_dim :]
    steps_dt = jax.nn.softplus(dt_raw + biases[None, :])
    decay_rate = -jnp.exp(rates)
    scanned = state_scan(x_act, steps_dt, decay_rate, b_mat, c_mat, skips, seg_ids)
    gated = scanned * jax.nn.silu(gate_in)
    scale = lax.rsqrt(jnp.mean(gated * gated, axis=1, keepdims=True) + EPS)
    return gated * scale * gate[None, :] * valid[:, None]


def right_product(left, right):
    return lax.dot_general(
        left, right, (((1,), (1,)), ((), ())), preferred_element_type=jnp.float32
    )


def left_product(left, right):
    return lax.dot_general(
        left, right, (((0,), (0,)), ((), ())), preferred_element_type=jnp.float32
    )


def local(
    hidden_in,
    lengths,
    norm_gain,
    in_proj,
    conv_weight,
    conv_bias,
    gate_gain,
    out_proj,
    decay_log,
    step_bias,
    skip_gain,
    grad_out,
):
    row_count = hidden_in.shape[0]
    gain_all, kernel_all, shift_all, gate_all, out_all = (
        lax.all_gather(norm_gain, ("fsdp", "dp"), axis=0, tiled=True),
        lax.all_gather(conv_weight, ("fsdp", "dp"), axis=0, tiled=True),
        lax.all_gather(conv_bias, ("fsdp", "dp"), axis=0, tiled=True),
        lax.all_gather(gate_gain, ("fsdp", "dp"), axis=0, tiled=True),
        lax.all_gather(out_proj, ("fsdp", "dp"), axis=0, tiled=True),
    )
    seg_ids, valid = segment_ids(lengths[0], row_count)
    x_float = hidden_in.astype(jnp.float32)
    normed32, norm_back = jax.vjp(pre_norm, x_float, gain_all.astype(jnp.float32))
    normed = normed32.astype(jnp.bfloat16)
    columns = normed
    projected = jnp.dot(
        columns,
        lax.all_gather(in_proj, ("fsdp", "dp"), axis=0, tiled=True),
        preferred_element_type=jnp.float32,
    )

    def branch(proj_in, kernel, shift_bias, gate, rates, biases, skips):
        return mixer_branch(proj_in, kernel, shift_bias, gate, rates, biases, skips, seg_ids, valid)

    mixed32, branch_back = jax.vjp(
        branch,
        projected,
        kernel_all.astype(jnp.float32),
        shift_all.astype(jnp.float32),
        gate_all.astype(jnp.float32),
        decay_log,
        step_bias,
        skip_gain,
    )
    mixed = mixed32.astype(jnp.bfloat16)
    hidden_out = (x_float + jnp.dot(mixed, out_all, preferred_element_type=jnp.float32)).astype(
        jnp.bfloat16
    )
    columns = mixed
    grad_out_proj = lax.psum_scatter(
        left_product(columns, grad_out), ("fsdp", "dp"), scatter_dimension=0, tiled=True
    )
    grad_mixed = right_product(
        grad_out, lax.all_gather(out_proj, ("fsdp", "dp"), axis=0, tiled=True)
    )
    grad_proj, grad_kernel, grad_shift, grad_gate, grad_rates, grad_biases, grad_skips = (
        branch_back(grad_mixed)
    )
    proj_low = grad_proj.astype(jnp.bfloat16)
    columns = normed
    grad_in_proj = lax.psum_scatter(
        left_product(columns, proj_low), ("fsdp", "dp"), scatter_dimension=0, tiled=True
    )
    grad_normed = right_product(
        proj_low, lax.all_gather(in_proj, ("fsdp", "dp"), axis=0, tiled=True)
    )
    grad_x, grad_gain = norm_back(grad_normed)
    grad_in = grad_out.astype(jnp.float32) + grad_x
    small_sums = (
        lax.psum_scatter(grad_gain, ("fsdp", "dp"), scatter_dimension=0, tiled=True),
        lax.psum_scatter(grad_kernel, ("fsdp", "dp"), scatter_dimension=0, tiled=True),
        lax.psum_scatter(grad_shift, ("fsdp", "dp"), scatter_dimension=0, tiled=True),
        lax.psum_scatter(grad_gate, ("fsdp", "dp"), scatter_dimension=0, tiled=True),
    )
    head_sums = lax.psum((grad_rates, grad_biases, grad_skips), ("fsdp", "dp"))
    return (
        hidden_out,
        grad_in,
        small_sums[0],
        grad_in_proj,
        small_sums[1],
        small_sums[2],
        small_sums[3],
        grad_out_proj,
        head_sums[0],
        head_sums[1],
        head_sums[2],
    )


def solution(mesh):
    in_specs = (
        P(("fsdp", "dp"), None),
        P(("fsdp", "dp"), None),
        P(("fsdp", "dp")),
        P(("fsdp", "dp"), None),
        P(("fsdp", "dp"), None),
        P(("fsdp", "dp")),
        P(("fsdp", "dp")),
        P(("fsdp", "dp"), None),
        P(),
        P(),
        P(),
        P(("fsdp", "dp"), None),
    )
    out_specs = (
        P(("fsdp", "dp"), None),
        P(("fsdp", "dp"), None),
        P(("fsdp", "dp")),
        P(("fsdp", "dp"), None),
        P(("fsdp", "dp"), None),
        P(("fsdp", "dp")),
        P(("fsdp", "dp")),
        P(("fsdp", "dp"), None),
        P(),
        P(),
        P(),
    )
    return jax.shard_map(local, mesh=mesh, in_specs=in_specs, out_specs=out_specs, check_vma=False)
```

profile of v0, /device:TPU:0, one launch (start us, length us, event | category | flops | bytes accessed | tf_op | source)
XLA Modules:
  0.0 1067.1 jit_solution(12854662397712302054)
XLA Ops:
  11.3 44.1 %all-reduce.29 = (bf16[1536]{0:T(1024)(128)(2,1)S(1)}, bf16[3328]{0:T(1024)(128)(2,1)S(1)}, bf16[3072]{0:T(1024)(128)(2,1)S(1)}) all-reduce(bf16[1536]{0:T(1024)(128)(2,1)S(1)} %dynamic-update-slice.1, bf16[3328]{0:T(1024)(128)(2,1)S(1)} %dynamic-update-slice, ...), channel_id=1, replica_groups=mesh['fsdp'=4,'dp'=8] {'fsdp','dp'}, use_global_device_ids=true, to_apply=%add.22 | all-reduce | flops 7936 | bytes 31744
  56.6 41.5 %all-gather = bf16[32,104,4]{1,2,0:T(4,128)(2,1)S(1)} all-gather(bf16[1,104,4]{1,2,0:T(4,128)(2,1)} %bitcast.141), channel_id=1, replica_groups=mesh['fsdp'=4,'dp'=8] {'fsdp','dp'}, dimensions={0}, use_global_device_ids=true | all-gather | bytes 27456 | tf_op jit(solution)/shard_map/all_gather | solution.py:134
  104.4 40.5 %all-gather.4.cloned.1.call-done = bf16[1536,6448]{1,0:T(8,128)(2,1)} async-done(((bf16[48,6448]{1,0:T(8,128)(2,1)}), bf16[1536,6448]{1,0:T(8,128)(2,1)}) %all-gather.4.cloned.1.call-update) | async-done | bytes 19808272 | tf_op jit(solution)/shard_map/all_gather | solution.py:146
  144.9 10.6 fusion.72
  167.7 4.8 fusion.32
  184.1 15.5 %fusion.38 = f32[256,48,64]{0,2,1:T(8,128)} fusion(f32[256,48,64]{0,2,1:T(8,128)S(1)} %bitcast.127, f32[256,48,64]{0,2,1:T(8,128)S(1)} %fusion.67, f32[48,256]{1,0:T(8,128)S(1)} %copy-done.30, f32[256,256]{1,0:T(8,128)S(1)} %fusion.89, f32[48,256]{1,0:T(8,128)S(1)} %copy_bitcast_fusion, pred[256,256]{1,0:T(8,128)(4,1)S(1)} %copy-done.23, ...), kind=kOutput, calls=%fused_computation.63 | convolution fusion | flops 2431647744 | bytes 9912512 | tf_op jit(solution)/shard_map/jvp()/while/body/eval_jaxpr/hts,shp->thp/dot_general | solution.py:58
  203.3 3.9 multiply_reduce_fusion.11
  209.7 18.0 %all-gather.6.cloned.1.call-done = bf16[3072,1536]{1,0:T(8,128)(2,1)} async-done(((bf16[96,1536]{1,0:T(8,128)(2,1)}), bf16[3072,1536]{1,0:T(8,128)(2,1)}) %all-gather.6.cloned.1.call-update) | async-done | bytes 9437200 | tf_op jit(solution)/shard_map/all_gather | solution.py:137
  227.7 6.6 multiply_reduce_fusion.8
  234.4 5.1 fusion.60
  251.5 6.8 multiply_reduce_fusion.7
  258.3 18.9 %fusion.11 = (f32[48,256]{1,0:T(8,128)S(1)}, f32[48,256]{1,0:T(8,128)S(1)}, f32[48,256]{1,0:T(8,128)S(1)}, f32[256,256]{1,0:T(8,128)S(1)}) fusion(f32[48,256]{1,0:T(8,128)S(1)} %copy.152, f32[256,256]{1,0:T(8,128)S(1)} %fusion.101, f32[48,256]{1,0:T(8,128)S(1)} %copy.148, pred[256,256]{1,0:T(8,128)(4,1)S(1)} %compare_and_fusion, ...), kind=kOutput, calls=%fused_computation.14 | convolution fusion | flops 2456711168 | bytes 7127040 | tf_op jit(solution)/shard_map/transpose(jvp())/while/body/eval_jaxpr/checkpoint/hts,shp->thp/dot_general | solution.py:58
  282.1 7.1 fusion.64
  289.3 13.4 %bitcast_add_fusion = f32[256,48,64]{0,2,1:T(8,128)} fusion(f32[256,48,64]{0,2,1:T(8,128)S(1)} %bitcast.126, f32[256,48,64]{0,2,1:T(8,128)} %get-tuple-element.199, f32[48,256]{1,0:T(8,128)S(1)} %copy.152, f32[256,256]{1,0:T(8,128)S(1)} %fusion.101, f32[48,256]{1,0:T(8,128)S(1)} %copy-done.29, pred[256,256]{1,0:T(8,128)(4,1)S(1)} %compare_and_fusion, ...), kind=kOutput, calls=%fused_computation.58 | convolution fusion | flops 2431647744 | bytes 9912512 | tf_op jit(solution)/shard_map/transpose(jvp())/while/body/eval_jaxpr/checkpoint/hts,shp->thp/dot_general | solution.py:58
  302.7 3.9 copy.159
  306.7 7.1 fusion.61
  314.8 7.1 fusion.95
  335.0 13.5 %fusion.54 = (f32[1536]{0:T(1024)}, f32[256]{0:T(256)S(1)}, f32[256,1536]{1,0:T(8,128)}) fusion(bf16[256,1536]{1,0:T(8,128)(2,1)} %param.12, f32[256]{0:T(256)S(1)} %fusion.83, f32[1536]{0:T(1024)S(1)} %convert_element_type.81, bf16[1536,6448]{1,0:T(8,128)(2,1)} %all-gather.4.cloned.1.call-done, f32[256,3072]{1,0:T(8,128)} %get-tuple-element.179, ...), kind=kOutput, calls=%fused_computation.87 | convolution fusion | flops 5078616064 | bytes 28784640 | tf_op jit(solution)/shard_map/dot_general | solution.py:106
  348.6 9.1 fusion.94
  357.8 18.9 %fusion.70 = f32[1536,6448]{1,0:T(8,128)} fusion(bf16[256,1536]{1,0:T(8,128)(2,1)} %param.12, f32[1536]{0:T(1024)S(1)} %convert_element_type.81, f32[256]{0:T(256)S(1)} %fusion.83, f32[256,3072]{1,0:T(8,128)} %get-tuple-element.179, f32[256,3328]{1,0:T(8,128)} %fusion.29, f32[256,48]{1,0:T(8,128)S(1)} %copy-done.18), kind=kOutput, calls=%fused_computation.108 | convolution fusion | flops 5077438464 | bytes 47012864 | tf_op jit(solution)/shard_map/dot_general | solution.py:112
  380.9 7.2 fusion.44
  388.1 84.8 %all-reduce.32.cloned.1.call-done = (f32[1536]{0:T(1024)}, f32[3328,4]{0,1:T(4,128)}, f32[3328]{0:T(1024)}, f32[3072]{0:T(1024)}, f32[48]{0:T(128)}, /*index=5*/f32[48]{0:T(128)}, f32[48]{0:T(128)}) async-done(((f32[1536]{0:T(1024)}, f32[3328,4]{0,1:T(4,128)}, f32[3328]{0:T(1024)}, f32[3072]{0:T(1024)}, f32[48]{0:T(128)}, /*index=5*/f32[48]{0:T(128)}, f32[48]{0:T(128)}), (f32[1536]{0:T(1024)}, ...) | async-done | bytes 85584
  478.1 209.4 %reduce-scatter.6.cloned.1.call-done = f32[96,1536]{1,0:T(8,128)} async-done(((f32[3072,1536]{1,0:T(8,128)}), f32[96,1536]{1,0:T(8,128)}) %reduce-scatter.6.cloned.1.call-update) | async-done | bytes 589840 | tf_op jit(solution)/shard_map/reduce_scatter | solution.py:168
  687.5 369.6 %reduce-scatter.4.cloned.1.call-done = f32[48,6448]{1,0:T(8,128)} async-done(((f32[1536,6448]{1,0:T(8,128)}), f32[48,6448]{1,0:T(8,128)}) %reduce-scatter.4.cloned.1.call-update) | async-done | bytes 1238032 | tf_op jit(solution)/shard_map/reduce_scatter | solution.py:179
  (199 shorter events, 84.3 us)
Async XLA Ops:
  7.2 137.7 %all-gather.4.cloned.1.call-start = ((), (), s32[]{:S(2)}) async-start(), calls=%async_computation.2 | async-start | bytes 20680704 | tf_op jit(solution)/shard_map/all_gather | solution.py:146
  7.9 219.8 %all-gather.6.cloned.1.call-start = ((), (), s32[]{:S(2)}) async-start(), calls=%async_computation.3 | async-start | bytes 9732096 | tf_op jit(solution)/shard_map/all_gather | solution.py:137
  8.7 464.2 %all-reduce.32.cloned.1.call-start = ((), (), s32[]{:S(2)}) async-start(), calls=%async_computation.6 | async-start | bytes 183296
  158.4 14.1 %copy-start.3 = (f32[256,3328]{1,0:T(8,128)}, f32[256,3328]{1,0:T(8,128)S(1)}, u32[]{:S(2)}) copy-start(f32[256,3328]{1,0:T(8,128)S(1)} %slice.107) | copy-start | bytes 10223620
  178.6 21.0 %copy-start.8 = (f32[256,3072]{0,1:T(8,128)}, f32[256,3072]{0,1:T(8,128)S(1)}, u32[]{:S(2)}) copy-start(f32[256,3072]{0,1:T(8,128)S(1)} %copy.138) | copy-start | bytes 9437188
  207.2 27.2 %copy-start.5 = (f32[256,3072]{1,0:T(8,128)}, f32[256,3072]{1,0:T(8,128)S(1)}, u32[]{:S(2)}) copy-start(f32[256,3072]{1,0:T(8,128)S(1)} %get-tuple-element.173) | copy-start | bytes 9437188
  209.7 41.4 %copy-start.15 = (f32[256,128]{1,0:T(8,128)}, f32[256,128]{1,0:T(8,128)S(1)}, u32[]{:S(2)}) copy-start(f32[256,128]{1,0:T(8,128)S(1)} %get-tuple-element.113) | copy-start | bytes 393220
  244.9 33.5 %copy-start.34 = (f32[256]{0:T(256)}, f32[256]{0:T(256)S(1)}, u32[]{:S(2)}) copy-start(f32[256]{0:T(256)S(1)} %get-tuple-element.192) | copy-start | bytes 3076
  251.0 27.4 %copy-start.13 = (f32[48,2,128]{0,2,1:T(8,128)}, f32[48,2,128]{0,2,1:T(8,128)S(1)}, u32[]{:S(2)}) copy-start(f32[48,2,128]{0,2,1:T(8,128)S(1)} %copy.147) | copy-start | bytes 147460
  251.1 7.2 copy-start.28
  278.2 11.0 %copy-start.14 = (f32[256,48]{1,0:T(8,128)}, f32[256,48]{1,0:T(8,128)S(1)}, u32[]{:S(2)}) copy-start(f32[256,48]{1,0:T(8,128)S(1)} %copy.166) | copy-start | bytes 147460
  278.3 10.9 %copy-start.41 = (f32[48]{0:T(128)}, f32[48]{0:T(128)S(1)}, u32[]{:S(2)}) copy-start(f32[48]{0:T(128)S(1)} %get-tuple-element.190) | copy-start | bytes 580
  278.6 10.7 copy-start.29
  278.6 10.7 copy-start.47
  282.1 7.1 copy-start.2
  306.6 7.2 copy-start.16
  306.6 8.2 copy-start.33
  306.7 8.1 copy-start.4
  335.0 13.6 %copy-start.6 = (f32[256,3072]{1,0:T(8,128)S(1)}, f32[256,3072]{1,0:T(8,128)}, u32[]{:S(2)}) copy-start(f32[256,3072]{1,0:T(8,128)} %copy-done.5) | copy-start | bytes 9437188
  335.0 13.6 %copy-start.21 = (f32[3072]{0:T(1024)S(1)}, f32[3072]{0:T(1024)}, u32[]{:S(2)}) copy-start(f32[3072]{0:T(1024)} %convert_element_type.89) | copy-start | bytes 36868
  335.0 13.6 %copy-start.32 = (f32[256]{0:T(256)S(1)}, f32[256]{0:T(256)}, u32[]{:S(2)}) copy-start(f32[256]{0:T(256)} %fusion.84) | copy-start | bytes 3076
  335.0 13.6 %copy-start.36 = (f32[256]{0:T(256)S(1)}, f32[256]{0:T(256)}, u32[]{:S(2)}) copy-start(f32[256]{0:T(256)} %get-tuple-element.193) | copy-start | bytes 3076
  348.5 338.9 %reduce-scatter.6.cloned.1.call-start = ((), (), s32[]{:S(2)}) async-start(), calls=%async_computation.5 | async-start | bytes 19464192 | tf_op jit(solution)/shard_map/reduce_scatter | solution.py:168
  357.8 699.2 %reduce-scatter.4.cloned.1.call-start = ((), (), s32[]{:S(2)}) async-start(), calls=%async_computation.4 | async-start | bytes 41361408 | tf_op jit(solution)/shard_map/reduce_scatter | solution.py:179
  (29 other events, 109.5 us)
Sparse Core Ops, SparseCore 0:
  11.0 133.8 all-gather.3
  147.9 79.7 all-gather.5
  348.7 124.1 all-reduce.31
  479.7 207.6 reduce-scatter.5
  694.3 362.6 reduce-scatter.3
where the time goes:
time: 1070 us
  waiting for transfers between devices  724 us (68%)
  matrix products  144 us (13%)
  blocking collectives  85.6 us (8%)
  other arithmetic  50.8 us (5%)
  local copies, waits for them, and re-layouts  47.5 us (4%)
  between operations  15.4 us (1%)
    reduce_scatter x1, waiting for transfers between devices, local(): lax.psum_scatter(left_product(columns, proj_low), ('fsdp', 'dp'), scatter...  370 us
    reduce_scatter x1, waiting for transfers between devices, local(): lax.psum_scatter(left_product(columns, grad_out), ('fsdp', 'dp'), scatter...  209 us
    unnamed x6, waiting for transfers between devices  86.2 us
    dot_general x3, matrix products, block_step(): result = jnp.einsum('hts,shp->thp', mixing, x_blk, precision=full_precision)  47.8 us
    unnamed x1, blocking collectives  44.1 us
    all_gather x1, blocking collectives, local(): lax.all_gather(conv_weight, ('fsdp', 'dp'), axis=0, tiled=True)  41.5 us
    all_gather x1, waiting for transfers between devices, local(): lax.all_gather(in_proj, ('fsdp', 'dp'), axis=0, tiled=True)  40.5 us
    dot_general x2, matrix products, left_product(): lax.dot_general(left, right, (((0,), (0,)), ((), ())), preferred_element_...  28.1 us
  transfers between devices with their start and end apart: 5, of which 5 were waited for; matrix products, arithmetic and copies ran while one was open for 11% of the time, Pallas kernels for 0%

commit v1 on v0

--- a/solution.py
+++ b/solution.py
@@ -143,7 +143,12 @@
     columns = normed
     projected = jnp.dot(
         columns,
-        lax.all_gather(in_proj, ("fsdp", "dp"), axis=0, tiled=True),
+        jnp.concatenate(
+            lax.all_to_all(
+                jnp.stack([in_proj] * lax.axis_size(("fsdp", "dp"))), ("fsdp", "dp"), 0, 0
+            ),
+            axis=0,
+        ),
         preferred_element_type=jnp.float32,
     )
 

time: 1070 us -> 1580 us (1.48)
  blocking collectives: 85.6 us -> 637 us
  waiting for transfers between devices: 724 us -> 667 us
    all_gather x1, blocking collectives: 41.5 us -> 599 us  [local(): lax.all_gather(conv_weight, ('fsdp', 'dp'), axis=0, tiled=True)]
    all_gather x1, waiting for transfers between devices: 40.5 us -> 0.01 us  [local(): lax.all_gather(in_proj, ('fsdp', 'dp'), axis=0, tiled=True)]
    all_gather x1, waiting for transfers between devices: 18 us -> 0.02 us  [local(): lax.all_gather(out_proj, ('fsdp', 'dp'), axis=0, tiled=True)]
  transfers between devices with their start and end apart: 5 -> 6, of which waited for: 5 -> 3; matrix products, arithmetic and copies ran while one was open for 11% -> 13% of each run, Pallas kernels for 0% -> 0%
where the time goes in v1:
time: 1580 us; the launch traced here: 1570 us
  waiting for transfers between devices  667 us (42%)
  blocking collectives  637 us (40%)
  matrix products  149 us (9%)
  local copies, waits for them, and re-layouts  46.6 us (3%)
  other arithmetic  42.8 us (3%)
  between operations  15.8 us (1%)
    all_gather x1, blocking collectives, local(): lax.all_gather(conv_weight, ('fsdp', 'dp'), axis=0, tiled=True)  599 us
    reduce_scatter x1, waiting for transfers between devices, local(): lax.psum_scatter(left_product(columns, proj_low), ('fsdp', 'dp'), scatter...  370 us
    reduce_scatter x1, waiting for transfers between devices, local(): lax.psum_scatter(left_product(columns, grad_out), ('fsdp', 'dp'), scatter...  209 us
    unnamed x6, waiting for transfers between devices  88.2 us
    dot_general x3, matrix products, block_step(): result = jnp.einsum('hts,shp->thp', mixing, x_blk, precision=full_precision)  52.5 us
    unnamed x1, blocking collectives  37.6 us
  transfers between devices with their start and end apart: 6, of which 3 were waited for; matrix products, arithmetic and copies ran while one was open for 13% of the time, Pallas kernels for 0%

profile of v1, /device:TPU:0, one launch (start us, length us, event | category | flops | bytes accessed | tf_op | source)
XLA Modules:
  0.0 1565.8 jit_solution(16890562832798359960)
XLA Ops:
  7.2 7.8 stack.2
  15.1 7.4 all-to-all-start
  24.1 599.4 %all-gather = bf16[32,104,4]{1,2,0:T(4,128)(2,1)S(1)} all-gather(bf16[1,104,4]{1,2,0:T(4,128)(2,1)S(1)} %bitcast.142), channel_id=1, replica_groups=mesh['fsdp'=4,'dp'=8] {'fsdp','dp'}, dimensions={0}, use_global_device_ids=true | all-gather | bytes 27456 | tf_op jit(solution)/shard_map/all_gather | solution.py:134
  624.4 37.6 %all-reduce.29 = (bf16[1536]{0:T(1024)(128)(2,1)S(1)}, bf16[3328]{0:T(1024)(128)(2,1)S(1)}, bf16[3072]{0:T(1024)(128)(2,1)S(1)}) all-reduce(bf16[1536]{0:T(1024)(128)(2,1)S(1)} %dynamic-update-slice.1, bf16[3328]{0:T(1024)(128)(2,1)S(1)} %dynamic-update-slice, ...), channel_id=1, replica_groups=mesh['fsdp'=4,'dp'=8] {'fsdp','dp'}, use_global_device_ids=true, to_apply=%add.22 | all-reduce | flops 7936 | bytes 31744
  665.8 9.8 fusion.72
  678.5 4.0 fusion.32
  696.4 16.6 %fusion.38 = f32[256,48,64]{0,2,1:T(8,128)} fusion(f32[256,48,64]{0,2,1:T(8,128)S(1)} %bitcast.128, f32[256,48,64]{0,2,1:T(8,128)S(1)} %fusion.67, f32[48,256]{1,0:T(8,128)S(1)} %copy-done.32, f32[256,256]{1,0:T(8,128)S(1)} %fusion.89, f32[48,256]{1,0:T(8,128)S(1)} %copy_bitcast_fusion, pred[256,256]{1,0:T(8,128)(4,1)} %compare_and_fusion.1, f32[48]{0:T(128)} %param.22, ...), kind=kOutput, calls=%fused_computation.63 | convolution fusion | flops 2431647744 | bytes 9912512 | tf_op jit(solution)/shard_map/jvp()/while/body/eval_jaxpr/hts,shp->thp/dot_general | solution.py:58
  716.6 3.9 multiply_reduce_fusion.11
  720.6 7.5 multiply_reduce_fusion.8
  728.1 5.1 fusion.60
  746.3 21.7 %fusion.11 = (f32[48,256]{1,0:T(8,128)}, f32[48,256]{1,0:T(8,128)}, f32[48,256]{1,0:T(8,128)}, f32[256,256]{1,0:T(8,128)}) fusion(f32[48,256]{1,0:T(8,128)} %copy.152, f32[256,256]{1,0:T(8,128)S(1)} %fusion.101, f32[48,256]{1,0:T(8,128)} %copy.148, pred[256,256]{1,0:T(8,128)(4,1)S(1)} %compare_and_fusion, f32[256,48,64]{0,2,1:T(8,128)} %bitcast.129, ...), kind=kOutput, calls=%fused_computation.14 | convolution fusion | flops 2456711168 | bytes 7127040 | tf_op jit(solution)/shard_map/transpose(jvp())/while/body/eval_jaxpr/checkpoint/hts,shp->thp/dot_general | solution.py:58
  770.0 4.2 multiply_reduce_fusion.9
  775.1 6.6 multiply_reduce_fusion.7
  783.4 14.1 bitcast_add_fusion
  804.3 7.1 fusion.64
  812.0 5.1 fusion.61
  817.6 6.6 fusion.95
  831.1 13.3 fusion.54
  844.6 9.1 fusion.94
  853.8 19.2 %fusion.70 = f32[1536,6448]{1,0:T(8,128)} fusion(bf16[256,1536]{1,0:T(8,128)(2,1)} %param.12, f32[1536]{0:T(1024)S(1)} %convert_element_type.81, f32[256]{0:T(256)S(1)} %fusion.83, f32[256,3072]{1,0:T(8,128)} %get-tuple-element.179, f32[256,3328]{1,0:T(8,128)} %fusion.29, f32[256,48]{1,0:T(8,128)S(1)} %get-tuple-element.170), kind=kOutput, calls=%fused_computation.108 | convolution fusion | flops 5077438464 | bytes 47012864 | tf_op jit(solution)/shard_map/dot_general | solution.py:112
  877.1 7.2 fusion.44
  884.4 86.8 %all-reduce.32.cloned.1.call-done = (f32[1536]{0:T(1024)}, f32[3328,4]{0,1:T(4,128)}, f32[3328]{0:T(1024)}, f32[3072]{0:T(1024)}, f32[48]{0:T(128)}, /*index=5*/f32[48]{0:T(128)}, f32[48]{0:T(128)}) async-done(((f32[1536]{0:T(1024)}, f32[3328,4]{0,1:T(4,128)}, f32[3328]{0:T(1024)}, f32[3072]{0:T(1024)}, f32[48]{0:T(128)}, /*index=5*/f32[48]{0:T(128)}, f32[48]{0:T(128)}), (f32[1536]{0:T(1024)}, ...) | async-done | bytes 85584
  976.3 209.4 %reduce-scatter.6.cloned.1.call-done = f32[96,1536]{1,0:T(8,128)} async-done(((f32[3072,1536]{1,0:T(8,128)}), f32[96,1536]{1,0:T(8,128)}) %reduce-scatter.6.cloned.1.call-update) | async-done | bytes 589840 | tf_op jit(solution)/shard_map/reduce_scatter | solution.py:173
  1185.7 369.6 %reduce-scatter.4.cloned.1.call-done = f32[48,6448]{1,0:T(8,128)} async-done(((f32[1536,6448]{1,0:T(8,128)}), f32[48,6448]{1,0:T(8,128)}) %reduce-scatter.4.cloned.1.call-update) | async-done | bytes 1238032 | tf_op jit(solution)/shard_map/reduce_scatter | solution.py:184
  (220 shorter events, 70.7 us)
Async XLA Ops:
  15.0 608.6 %copy-start.50 = (bf16[48]{0:T(256)(128)(2,1)S(1)}, bf16[48]{0:T(256)(128)(2,1)}, u32[]{:S(2)}) copy-start(bf16[48]{0:T(256)(128)(2,1)} %param.14) | copy-start | bytes 292
  15.0 608.8 %copy-start.51 = (bf16[104]{0:T(256)(128)(2,1)S(1)}, bf16[104]{0:T(256)(128)(2,1)}, u32[]{:S(2)}) copy-start(bf16[104]{0:T(256)(128)(2,1)} %param.17) | copy-start | bytes 628
  15.0 609.1 %copy-start.52 = (bf16[96]{0:T(256)(128)(2,1)S(1)}, bf16[96]{0:T(256)(128)(2,1)}, u32[]{:S(2)}) copy-start(bf16[96]{0:T(256)(128)(2,1)} %param.18) | copy-start | bytes 580
  15.0 647.5 %copy-start.53 = (s32[1,4]{1,0:T(1,128)S(1)}, s32[1,4]{1,0:T(1,128)}, u32[]{:S(2)}) copy-start(s32[1,4]{1,0:T(1,128)} %param.13) | copy-start | bytes 52
  15.1 648.5 %copy-start.11 = (bf16[256,1536]{1,0:T(8,128)(2,1)S(1)}, bf16[256,1536]{1,0:T(8,128)(2,1)}, u32[]{:S(2)}) copy-start(bf16[256,1536]{1,0:T(8,128)(2,1)} %param.12) | copy-start | bytes 2359300
  15.1 648.8 %copy-start.55 = (f32[48]{0:T(128)S(1)}, f32[48]{0:T(128)}, u32[]{:S(2)}) copy-start(f32[48]{0:T(128)} %param.20) | copy-start | bytes 580
  15.1 650.7 %all-to-all-start = ((bf16[32,48,6448]{2,1,0:T(8,128)(2,1)}), bf16[32,48,6448]{2,1,0:T(8,128)(2,1)}, u32[]{:S(2)}, u32[]{:S(2)}) async-start(bf16[32,48,6448]{2,1,0:T(8,128)(2,1)} %stack.2), calls=%async_computation | async-start | bytes 40108032 | tf_op jit(solution)/shard_map/all_to_all | solution.py:147
  22.5 698.0 %all-gather.4.cloned.1.call-start = ((), (), s32[]{:S(2)}) async-start(), calls=%async_computation.3 | async-start | bytes 9732096 | tf_op jit(solution)/shard_map/all_gather | solution.py:137
  23.3 807.8 %all-gather.6.cloned.1.call-start = ((), (), s32[]{:S(2)}) async-start(), calls=%async_computation.4 | async-start | bytes 20680704 | tf_op jit(solution)/shard_map/all_gather | solution.py:188
  24.0 947.2 %all-reduce.32.cloned.1.call-start = ((), (), s32[]{:S(2)}) async-start(), calls=%async_computation.7 | async-start | bytes 183296
  663.6 14.8 copy-start.19
  663.6 14.8 copy-start.21
  663.6 14.8 copy-start.23
  663.6 14.8 copy-start.25
  664.5 24.1 %copy-start.45 = (f32[48]{0:T(128)}, f32[48]{0:T(128)S(1)}, u32[]{:S(2)}) copy-start(f32[48]{0:T(128)S(1)} %exponential_negate_fusion) | copy-start | bytes 580
  688.6 24.4 %copy-start.7 = (f32[256,3072]{0,1:T(8,128)}, f32[256,3072]{0,1:T(8,128)S(1)}, u32[]{:S(2)}) copy-start(f32[256,3072]{0,1:T(8,128)S(1)} %copy.138) | copy-start | bytes 9437188
  735.6 32.5 %copy-start = (f32[256,3072]{0,1:T(8,128)}, f32[256,3072]{0,1:T(8,128)S(1)}, u32[]{:S(2)}) copy-start(f32[256,3072]{0,1:T(8,128)S(1)} %copy.145) | copy-start | bytes 9437188
  745.0 23.1 %copy-start.27 = (pred[256,256]{1,0:T(8,128)(4,1)}, pred[256,256]{1,0:T(8,128)(4,1)S(1)}, u32[]{:S(2)}) copy-start(pred[256,256]{1,0:T(8,128)(4,1)S(1)} %compare_and_fusion) | copy-start | bytes 196612
  746.3 21.7 %copy-start.15 = (f32[256,256]{1,0:T(8,128)}, f32[256,256]{1,0:T(8,128)S(1)}, u32[]{:S(2)}) copy-start(f32[256,256]{1,0:T(8,128)S(1)} %fusion.101) | copy-start | bytes 786436
  831.1 13.4 copy-start.18
  831.1 13.5 copy-start.34
  831.1 13.5 copy-start.42
  844.5 341.3 %reduce-scatter.6.cloned.1.call-start = ((), (), s32[]{:S(2)}) async-start(), calls=%async_computation.6 | async-start | bytes 19464192 | tf_op jit(solution)/shard_map/reduce_scatter | solution.py:173
  853.7 701.6 %reduce-scatter.4.cloned.1.call-start = ((), (), s32[]{:S(2)}) async-start(), calls=%async_computation.5 | async-start | bytes 41361408 | tf_op jit(solution)/shard_map/reduce_scatter | solution.py:184
  (39 other events, 247.3 us)
Sparse Core Ops, SparseCore 0:
  26.4 181.5 all-gather.3
  211.0 297.4 all-gather.5
  844.6 126.5 all-reduce.31
  978.0 207.6 reduce-scatter.5
  1192.6 362.6 reduce-scatter.3
